TPU v7x, 32 devices: a whole 2x2x4 slice. The times are simulated.
32 devices in a mesh: row: 8 (over z, x), col: 4 (over y, core).
Axes of the slice: x: 2, y: 2, z: 4, core: 2. Of those that a mesh axis runs over, the one named last changes fastest.
Arguments:
- basis_blocks: float32 [8, 16, 262144], P(None, None, ('col', 'row')), may hold values from -6 to 6
- tile_values: bfloat16 [4, 8, 384, 128, 128], P('col', 'row'), may hold values from -0.375 to 0.375
- tile_rows: int32 [4, 8, 384], P('col', 'row'), may hold values from 0 to 511
- tile_column: int32 [4, 8, 384], P('col', 'row'), may hold values from 0 to 255
- tile_count: int32 [4, 8], P('col', 'row'), may hold values from 1 to 384, as said below
- diagonal: float32 [262144], P(('col', 'row')), may hold values from 1 to 6
Outputs:
- new_block: float32 [16, 262144], P(None, ('col', 'row'))
- coefficients: float32 [8, 16, 16], replicated
- triangle: float32 [16, 16], replicated
Inputs may be any that keep to these rules, and one draw needn't show every extreme that they name: Each operator block stores tile_count tiles in its first slots; at most 384, and some block has exactly 384 in every draw. Slots past the count hold arbitrary data and are ignored.
All inputs are finite; a program needn't handle non-finite values.
Results may differ from a plain program's by a relative error of at most 0.0031.
Values may be sent and summed in bfloat16 or wider, within the bound.
A program may use at most 128 MiB of HBM per device.

v0:
```python
import jax
import jax.numpy as jnp
from jax import lax
from jax.sharding import PartitionSpec as P


def local(basis_blocks, tile_values, tile_rows, tile_column, tile_count, diagonal):
    rhs_width = basis_blocks.shape[1]
    seg_rows = basis_blocks.shape[2]
    total_rows = seg_rows * lax.axis_size("row") * lax.axis_size("col")
    block_tiles = lax.axis_size("row") * seg_rows // 128
    vector = basis_blocks[-1].astype(jnp.bfloat16)
    expanded = lax.all_gather(vector, "col", axis=1, tiled=True)
    xblocks = expanded.reshape(rhs_width, -1, 128)
    values = tile_values[0, 0]
    row_ids = tile_rows[0, 0]
    column_ids = tile_column[0, 0]
    live_count = tile_count[0, 0]
    live_tiles = jnp.arange(values.shape[0], dtype=jnp.int32) < live_count
    gathered = jnp.take(xblocks, column_ids, axis=1)
    products = jnp.einsum("stj,tji->tsi", gathered, values, preferred_element_type=jnp.float32)
    inside = live_tiles & (row_ids >= 0) & (row_ids < 0 + block_tiles)
    segment_ids = jnp.where(inside, row_ids - 0, block_tiles)
    summed = jax.ops.segment_sum(products, segment_ids, num_segments=block_tiles + 1)
    folded = lax.psum_scatter(summed[:block_tiles], "row", scatter_dimension=0, tiled=True)
    image_rows = folded.transpose(1, 0, 2).reshape(rhs_width, seg_rows)
    image_rows = image_rows + diagonal[None, :] * basis_blocks[-1]
    highest = lax.Precision.HIGHEST
    local_proj = jnp.einsum("kap,bp->kab", basis_blocks, image_rows, precision=highest)
    local_self = jnp.dot(image_rows, image_rows.T, precision=highest)
    local_basis = jnp.einsum("kap,lcp->kalc", basis_blocks, basis_blocks, precision=highest)
    proj_sum, image_sum, basis_sum = lax.psum((local_proj, local_self, local_basis), ("row", "col"))
    coefficients = proj_sum / total_rows
    image_gram = image_sum / total_rows
    basis_gram = basis_sum / total_rows
    projected = image_rows - jnp.einsum(
        "kab,kap->bp", coefficients, basis_blocks, precision=highest
    )
    cross_term = jnp.einsum("kab,kad->bd", coefficients, coefficients, precision=highest)
    basis_term = jnp.einsum(
        "kab,kalc,lcd->bd", coefficients, basis_gram, coefficients, precision=highest
    )
    gram_matrix = image_gram - 2.0 * cross_term + basis_term
    lower_factor = jnp.linalg.cholesky(gram_matrix)
    new_block = lax.linalg.triangular_solve(lower_factor, projected, left_side=True, lower=True)
    return (new_block, coefficients, lower_factor.T)


def solution(mesh):
    in_specs = (
        P(None, None, ("col", "row")),
        P("col", "row", None, None, None),
        P("col", "row", None),
        P("col", "row", None),
        P("col", "row"),
        P(("col", "row")),
    )
    out_specs = (P(None, ("col", "row")), P(), P())
    return jax.shard_map(local, mesh=mesh, in_specs=in_specs, out_specs=out_specs, check_vma=False)
```

profile of v0, /device:TPU:0, one launch (start us, length us, event | category | flops | bytes accessed | tf_op | source)
XLA Modules:
  0.0 285.5 jit_solution(4340497072909810050)
XLA Ops:
  8.0 0.0 all-gather.2.cloned.1.call-start
  8.0 1.8 bitcast_convert_fusion
  9.8 0.0 all-gather.2.cloned.1.call-update
  9.8 0.0 reduce-scatter.2.cloned.1.call-start
  10.5 0.7 reduce.7
  11.2 0.7 fusion.22
  11.9 0.7 fusion.23
  12.7 17.7 %all-gather.2.cloned.1.call-done = bf16[16,32768]{1,0:T(8,128)(2,1)} async-done(((bf16[16,8192]{1,0:T(8,128)(2,1)}), bf16[16,32768]{1,0:T(8,128)(2,1)}) %all-gather.2.cloned.1.call-update) | async-done | bytes 1048592 | tf_op jit(solution)/shard_map/all_gather | solution.py:13
  30.4 1.4 copy_bitcast_fusion
  31.8 2.6 gather_fusion
  34.4 6.9 %fusion = f32[384,16,128]{2,1,0:T(8,128)S(1)} fusion(bf16[1,1,384,128,128]{4,3,2,1,0:T(8,128)(2,1)} %param.7, bf16[384,16,128]{2,1,0:T(8,128)(2,1)} %gather_fusion, pred[384]{0:T(512)(128)(4,1)S(1)} %compare_and_fusion), kind=kOutput, calls=%fused_computation.2 | convolution fusion | flops 202113024 | bytes 17301888 | tf_op jit(solution)/shard_map/stj,tji->tsi/dot_general | solution.py:21
  41.2 2.2 broadcast_in_dim.19
  43.5 51.1 %scatter_fusion = f32[513,16,128]{2,1,0:T(8,128)} fusion(f32[513,16,128]{2,1,0:T(8,128)} %broadcast_in_dim.19, s32[384]{0:T(512)S(1)} %fusion.23, f32[384,16,128]{2,1,0:T(8,128)S(1)} %fusion), kind=kCustom, calls=%fused_computation.1 | custom fusion | flops 786432 | bytes 9438720 | tf_op jit(solution)/shard_map/scatter-add | solution.py:24
  94.6 4.4 %slice.21 = f32[512,16,128]{2,1,0:T(8,128)} slice(f32[513,16,128]{2,1,0:T(8,128)} %scatter_fusion), slice={[0:512], [0:16], [0:128]} | slice | bytes 8388608 | tf_op jit(solution)/shard_map/slice | solution.py:25
  99.0 0.0 reduce-scatter.2.cloned.1.call-update
  99.0 0.0 copy-start.1
  99.0 0.2 all-reduce.3.cloned.1.call-start
  99.3 18.0 %fusion.3 = f32[8,16,8,16]{3,1,2,0:T(8,128)} fusion(f32[8,16,8192]{2,1,0:T(8,128)} %param.6), kind=kOutput, calls=%fused_computation.6 | convolution fusion | flops 1610612736 | bytes 4259840 | tf_op jit(solution)/shard_map/kap,lcp->kalc/dot_general | solution.py:31
  117.3 0.0 all-reduce.3.cloned.1.call-update
  117.3 1.1 slice_bitcast_fusion
  118.4 0.1 copy.61
  118.5 70.4 %reduce-scatter.2.cloned.1.call-done = f32[64,16,128]{2,1,0:T(8,128)} async-done(((f32[512,16,128]{2,1,0:T(8,128)}), f32[64,16,128]{2,1,0:T(8,128)}) %reduce-scatter.2.cloned.1.call-update) | async-done | bytes 524304 | tf_op jit(solution)/shard_map/reduce_scatter | solution.py:25
  188.9 0.0 copy-done.1
  188.9 0.0 copy-start
  188.9 17.2 %convolution_bitcast_fusion.1 = f32[8,16,16]{1,2,0:T(8,128)S(1)} fusion(f32[8,16,8192]{2,1,0:T(8,128)} %param.6, f32[8192]{0:T(1024)S(1)} %copy-done.1, f32[64,16,128]{2,1,0:T(8,128)} %reduce-scatter.2.cloned.1.call-done), kind=kOutput, calls=%fused_computation.12 | convolution fusion | flops 201588736 | bytes 5283840 | tf_op jit(solution)/shard_map/kap,bp->kab/dot_general | solution.py:29
  206.1 0.0 copy-done
  206.1 1.0 convolution_bitcast_fusion.5
  207.1 41.0 %all-reduce = (f32[8,16,16]{1,2,0:T(8,128)S(1)}, f32[16,16]{0,1:T(8,128)S(1)}) all-reduce(f32[8,16,16]{1,2,0:T(8,128)S(1)} %convolution_bitcast_fusion.1, f32[16,16]{0,1:T(8,128)S(1)} %convolution_bitcast_fusion.5), channel_id=1, replica_groups=mesh['row'=8,'col'=4] {'row','col'}, use_global_device_ids=true, to_apply=%region_3.4 | all-reduce | flops 2304 | bytes 18432 | tf_op jit(solution)/shard_map/psum | solution.py:32
  248.1 14.4 %all-reduce.3.cloned.1.call-done = f32[8,16,8,16]{3,1,2,0:T(8,128)} async-done(((f32[8,16,8,16]{3,1,2,0:T(8,128)}), f32[8,16,8,16]{3,1,2,0:T(8,128)}) %all-reduce.3.cloned.1.call-update) | async-done | bytes 65552 | tf_op jit(solution)/shard_map/psum | solution.py:32
  262.5 1.4 convolution_bitcast_fusion.2
  263.9 0.2 convolution_bitcast_fusion.3
  264.1 0.2 fusion.11
  264.3 0.1 copy.40
  264.4 1.5 cholesky.16
  265.9 0.6 compare_reduce_fusion
  266.6 0.6 fusion.21
  267.2 1.2 custom-call.6
  268.5 0.7 copy.42
  269.1 0.7 copy.41
  269.9 6.7 %fusion.2 = f32[16,8192]{1,0:T(8,128)S(1)} fusion(f32[8,16,8192]{2,1,0:T(8,128)} %param.6, f32[8192]{0:T(1024)S(1)} %copy-done.1, f32[8,16,16]{1,2,0:T(8,128)S(1)} %get-tuple-element.12, f32[64,16,128]{2,1,0:T(8,128)S(1)} %copy-done), kind=kOutput, calls=%fused_computation.5 | convolution fusion | flops 201721856 | bytes 5808128 | tf_op jit(solution)/shard_map/kab,kap->bp/dot_general | solution.py:36
  276.6 1.4 fusion.18
  (5 shorter events, 0.1 us)
Async XLA Ops:
  8.0 22.4 %all-gather.2.cloned.1.call-start = ((), (), s32[]{:S(2)}) async-start(), calls=%async_computation.1 | async-start | bytes 1310720 | tf_op jit(solution)/shard_map/all_gather | solution.py:13
  9.8 179.0 %reduce-scatter.2.cloned.1.call-start = ((), (), s32[]{:S(2)}) async-start(), calls=%async_computation.2 | async-start | bytes 4718592 | tf_op jit(solution)/shard_map/reduce_scatter | solution.py:25
  99.0 89.8 %copy-start.1 = (f32[8192]{0:T(1024)S(1)}, f32[8192]{0:T(1024)}, u32[]{:S(2)}) copy-start(f32[8192]{0:T(1024)} %param.11) | copy-start | bytes 98308
  99.0 163.4 %all-reduce.3.cloned.1.call-start = ((), (), s32[]{:S(2)}) async-start(), calls=%async_computation.3 | async-start | bytes 1048576 | tf_op jit(solution)/shard_map/psum | solution.py:32
  188.9 17.2 %copy-start = (f32[64,16,128]{2,1,0:T(8,128)S(1)}, f32[64,16,128]{2,1,0:T(8,128)}, u32[]{:S(2)}) copy-start(f32[64,16,128]{2,1,0:T(8,128)} %reduce-scatter.2.cloned.1.call-done) | copy-start | bytes 1572868
Sparse Core Ops, SparseCore 0:
  10.9 19.4 all-gather.1
  99.1 89.6 reduce-scatter.1
Sparse Core Ops, SparseCore 1:
  117.4 145.0 all-reduce.2
where the time goes:
time: 288 us; the launch traced here: 285 us
  waiting for transfers between devices  103 us (36%)
  other arithmetic  57.3 us (20%)
  matrix products  53.1 us (18%)
  blocking collectives  41 us (14%)
  between operations  16.2 us (6%)
  local copies, waits for them, and re-layouts  15.1 us (5%)
    reduce_scatter x1, waiting for transfers between devices, local(): lax.psum_scatter(summed[:block_tiles], 'row', scatter_dimension=0, tiled=...  70.4 us
    scatter-add x1, other arithmetic, local(): jax.ops.segment_sum(products, segment_ids, num_segments=block_tiles + 1)  51.1 us
    psum x1, blocking collectives, local(): lax.psum((local_proj, local_self, local_basis), ('row', 'col'))  41 us
    dot_general x1, matrix products, local(): jnp.einsum('kap,lcp->kalc', basis_blocks, basis_blocks, precision=highest)  18 us
    all_gather x1, waiting for transfers between devices, local(): expanded = lax.all_gather(vector, 'col', axis=1, tiled=True)  17.7 us
    dot_general x1, matrix products, local(): jnp.einsum('kap,bp->kab', basis_blocks, image_rows, precision=highest)  17.2 us
    psum x1, waiting for transfers between devices, local(): lax.psum((local_proj, local_self, local_basis), ('row', 'col'))  14.4 us
    dot_general x1, matrix products, local(): jnp.einsum('stj,tji->tsi', gathered, values, preferred_element_type=jnp.f...  6.87 us
  transfers between devices with their start and end apart: 3, of which 3 were waited for; matrix products, arithmetic and copies ran while one was open for 14% of the time, Pallas kernels for 0%

commit v1 on v0

--- a/solution.py
+++ b/solution.py
@@ -29,7 +29,9 @@
     local_proj = jnp.einsum("kap,bp->kab", basis_blocks, image_rows, precision=highest)
     local_self = jnp.dot(image_rows, image_rows.T, precision=highest)
     local_basis = jnp.einsum("kap,lcp->kalc", basis_blocks, basis_blocks, precision=highest)
-    proj_sum, image_sum, basis_sum = lax.psum((local_proj, local_self, local_basis), ("row", "col"))
+    proj_sum, image_sum, basis_sum = lax.psum(
+        lax.psum((local_proj, local_self, local_basis), "col"), "row"
+    )
     coefficients = proj_sum / total_rows
     image_gram = image_sum / total_rows
     basis_gram = basis_sum / total_rows

time: 288 us -> 287 us (level)
  blocking collectives: 41 us -> 48.9 us
  waiting for transfers between devices: 103 us -> 98.1 us
    reduce_scatter x1, waiting for transfers between devices: 70.4 us -> 88.1 us  [local(): lax.psum_scatter(summed[:block_tiles], 'row', scatter_dimension=0, tiled=...]
    all_gather x1, waiting for transfers between devices: 17.7 us -> 1.06 us  [local(): expanded = lax.all_gather(vector, 'col', axis=1, tiled=True)]
    psum x1 -> x2, blocking collectives: 41 us -> 48.9 us  [the longest x1 37.5 us: local(): lax.psum(lax.psum((local_proj, local_self, local_basis), 'col'), 'row')]
    psum x1 -> x2, waiting for transfers between devices: 14.4 us -> 8.87 us  [the longest x1 8.85 us: local(): lax.psum(lax.psum((local_proj, local_self, local_basis), 'col'), 'row')]
  transfers between devices with their start and end apart: 3 -> 4, of which waited for: 3 -> 3; matrix products, arithmetic and copies ran while one was open for 14% -> 37% of each run, Pallas kernels for 0% -> 0%
where the time goes in v1:
time: 287 us; the launch traced here: 285 us
  waiting for transfers between devices  98.1 us (34%)
  other arithmetic  55.2 us (19%)
  matrix products  53.1 us (19%)
  blocking collectives  48.9 us (17%)
  local copies, waits for them, and re-layouts  15.1 us (5%)
  between operations  14.6 us (5%)
    reduce_scatter x1, waiting for transfers between devices, local(): lax.psum_scatter(summed[:block_tiles], 'row', scatter_dimension=0, tiled=...  88.1 us
    scatter-add x1, other arithmetic, local(): jax.ops.segment_sum(products, segment_ids, num_segments=block_tiles + 1)  51.1 us
    psum x1, blocking collectives, local(): lax.psum(lax.psum((local_proj, local_self, local_basis), 'col'), 'row')  37.5 us
    dot_general x1, matrix products, local(): jnp.einsum('kap,lcp->kalc', basis_blocks, basis_blocks, precision=highest)  18 us
    dot_general x1, matrix products, local(): jnp.einsum('kap,bp->kab', basis_blocks, image_rows, precision=highest)  17.1 us
    psum x1, blocking collectives, local(): lax.psum((local_proj, local_self, local_basis), 'col')  11.5 us
    psum x1, waiting for transfers between devices, local(): lax.psum(lax.psum((local_proj, local_self, local_basis), 'col'), 'row')  8.85 us
    dot_general x1, matrix products, local(): jnp.einsum('stj,tji->tsi', gathered, values, preferred_element_type=jnp.f...  6.97 us
  transfers between devices with their start and end apart: 4, of which 3 were waited for; matrix products, arithmetic and copies ran while one was open for 37% of the time, Pallas kernels for 0%

profile of v1, /device:TPU:0, one launch (start us, length us, event | category | flops | bytes accessed | tf_op | source)
XLA Modules:
  0.0 285.4 jit_solution(2259027449141796488)
XLA Ops:
  7.2 0.0 all-gather.2.cloned.1.call-start
  7.2 1.8 bitcast_convert_fusion
  9.0 0.0 all-gather.2.cloned.1.call-update
  9.0 0.0 copy-start.2
  9.0 0.0 copy-start.3
  9.0 0.0 all-reduce.5.cloned.1.call-start
  9.1 18.0 %fusion.3 = f32[8,16,8,16]{3,1,2,0:T(8,128)} fusion(f32[8,16,8192]{2,1,0:T(8,128)} %param.6), kind=kOutput, calls=%fused_computation.6 | convolution fusion | flops 1610612736 | bytes 4259840 | tf_op jit(solution)/shard_map/kap,lcp->kalc/dot_general | solution.py:31
  27.1 0.0 all-reduce.5.cloned.1.call-update
  27.1 0.0 reduce-scatter.2.cloned.1.call-start
  27.2 0.0 copy-done.2
  27.9 0.0 copy-done.3
  27.9 1.1 all-gather.2.cloned.1.call-done
  29.0 1.4 copy_bitcast_fusion
  30.4 2.6 gather_fusion
  33.0 7.0 %fusion = f32[384,16,128]{2,1,0:T(8,128)S(1)} fusion(bf16[1,1,384,128,128]{4,3,2,1,0:T(8,128)(2,1)} %param.7, bf16[384,16,128]{2,1,0:T(8,128)(2,1)} %gather_fusion, pred[384]{0:T(512)(128)(4,1)S(1)} %compare_and_fusion), kind=kOutput, calls=%fused_computation.2 | convolution fusion | flops 202113024 | bytes 17301888 | tf_op jit(solution)/shard_map/stj,tji->tsi/dot_general | solution.py:21
  39.9 2.2 broadcast_in_dim.19
  42.2 51.1 %scatter_fusion = f32[513,16,128]{2,1,0:T(8,128)} fusion(f32[513,16,128]{2,1,0:T(8,128)} %broadcast_in_dim.19, s32[384]{0:T(512)S(1)} %fusion.23, f32[384,16,128]{2,1,0:T(8,128)S(1)} %fusion), kind=kCustom, calls=%fused_computation.1 | custom fusion | flops 786432 | bytes 9438720 | tf_op jit(solution)/shard_map/scatter-add | solution.py:24
  93.3 4.4 %slice.21 = f32[512,16,128]{2,1,0:T(8,128)} slice(f32[513,16,128]{2,1,0:T(8,128)} %scatter_fusion), slice={[0:512], [0:16], [0:128]} | slice | bytes 8388608 | tf_op jit(solution)/shard_map/slice | solution.py:25
  97.7 0.0 copy-start.1
  97.7 0.0 reduce-scatter.2.cloned.1.call-update
  97.7 0.2 all-reduce.7.cloned.1.call-start
  98.0 1.1 slice_bitcast_fusion
  99.0 0.1 copy.61
  99.2 0.0 all-reduce.5.cloned.1.call-done
  99.2 0.0 all-reduce.7.cloned.1.call-update
  99.2 88.1 %reduce-scatter.2.cloned.1.call-done = f32[64,16,128]{2,1,0:T(8,128)} async-done(((f32[512,16,128]{2,1,0:T(8,128)}), f32[64,16,128]{2,1,0:T(8,128)}) %reduce-scatter.2.cloned.1.call-update) | async-done | bytes 524304 | tf_op jit(solution)/shard_map/reduce_scatter | solution.py:25
  187.4 0.0 copy-done.1
  187.4 0.0 copy-start
  187.4 17.1 %convolution_bitcast_fusion.1 = f32[8,16,16]{1,2,0:T(8,128)S(1)} fusion(f32[8,16,8192]{2,1,0:T(8,128)} %param.6, f32[8192]{0:T(1024)S(1)} %copy-done.1, f32[64,16,128]{2,1,0:T(8,128)} %reduce-scatter.2.cloned.1.call-done), kind=kOutput, calls=%fused_computation.12 | convolution fusion | flops 201588736 | bytes 5283840 | tf_op jit(solution)/shard_map/kap,bp->kab/dot_general | solution.py:29
  204.5 0.0 copy-done
  204.5 1.0 convolution_bitcast_fusion.5
  205.5 11.5 %all-reduce.1 = (f32[8,16,16]{1,2,0:T(8,128)S(1)}, f32[16,16]{0,1:T(8,128)S(1)}) all-reduce(f32[8,16,16]{1,2,0:T(8,128)S(1)} %convolution_bitcast_fusion.1, f32[16,16]{0,1:T(8,128)S(1)} %convolution_bitcast_fusion.5), channel_id=1, replica_groups=mesh['row'=8,'col'=4] {'col'}, use_global_device_ids=true, to_apply=%region_4.5 | all-reduce | flops 2304 | bytes 18432 | tf_op jit(solution)/shard_map/psum | solution.py:33
  217.0 37.5 %all-reduce = (f32[8,16,16]{1,2,0:T(8,128)S(1)}, f32[16,16]{0,1:T(8,128)S(1)}) all-reduce(f32[8,16,16]{1,2,0:T(8,128)S(1)} %get-tuple-element.14, f32[16,16]{0,1:T(8,128)S(1)} %get-tuple-element.15), channel_id=1, replica_groups=mesh['row'=8,'col'=4] {'row'}, use_global_device_ids=true, to_apply=%region_5.6 | all-reduce | flops 2304 | bytes 18432 | tf_op jit(solution)/shard_map/psum | solution.py:32
  254.4 8.9 %all-reduce.7.cloned.1.call-done = f32[8,16,8,16]{3,1,2,0:T(8,128)} async-done(((f32[8,16,8,16]{3,1,2,0:T(8,128)}), f32[8,16,8,16]{3,1,2,0:T(8,128)}) %all-reduce.7.cloned.1.call-update) | async-done | bytes 65552 | tf_op jit(solution)/shard_map/psum | solution.py:32
  263.3 1.4 convolution_bitcast_fusion.2
  264.7 0.2 convolution_bitcast_fusion.3
  264.9 0.2 fusion.11
  265.1 0.1 copy.40
  265.2 1.5 cholesky.16
  266.7 0.6 compare_reduce_fusion
  267.4 0.6 fusion.21
  268.0 1.2 custom-call.6
  269.3 0.7 copy.42
  270.0 0.7 copy.41
  270.7 6.7 %fusion.2 = f32[16,8192]{1,0:T(8,128)S(1)} fusion(f32[8,16,8192]{2,1,0:T(8,128)} %param.6, f32[8192]{0:T(1024)S(1)} %copy-done.1, f32[8,16,16]{1,2,0:T(8,128)S(1)} %get-tuple-element.12, f32[64,16,128]{2,1,0:T(8,128)S(1)} %copy-done), kind=kOutput, calls=%fused_computation.5 | convolution fusion | flops 201721856 | bytes 5808128 | tf_op jit(solution)/shard_map/kab,kap->bp/dot_general | solution.py:38
  277.4 1.4 fusion.18
  (8 shorter events, 0.1 us)
Async XLA Ops:
  7.2 21.8 %all-gather.2.cloned.1.call-start = ((), (), s32[]{:S(2)}) async-start(), calls=%async_computation.1 | async-start | bytes 1310720 | tf_op jit(solution)/shard_map/all_gather | solution.py:13
  9.0 18.2 %copy-start.2 = (s32[1,1,384]{2,1,0:T(1,128)S(1)}, s32[1,1,384]{2,1,0:T(1,128)}, u32[]{:S(2)}) copy-start(s32[1,1,384]{2,1,0:T(1,128)} %param.9) | copy-start | bytes 4612
  9.0 18.9 %copy-start.3 = (s32[1,1,384]{2,1,0:T(1,128)S(1)}, s32[1,1,384]{2,1,0:T(1,128)}, u32[]{:S(2)}) copy-start(s32[1,1,384]{2,1,0:T(1,128)} %param.8) | copy-start | bytes 4612
  9.0 90.1 %all-reduce.5.cloned.1.call-start = ((), (), s32[]{:S(2)}) async-start(), calls=%async_computation.3 | async-start | bytes 1048576 | tf_op jit(solution)/shard_map/psum | solution.py:33
  27.1 160.2 %reduce-scatter.2.cloned.1.call-start = ((), (), s32[]{:S(2)}) async-start(), calls=%async_computation.2 | async-start | bytes 4718592 | tf_op jit(solution)/shard_map/reduce_scatter | solution.py:25
  97.7 89.7 %copy-start.1 = (f32[8192]{0:T(1024)S(1)}, f32[8192]{0:T(1024)}, u32[]{:S(2)}) copy-start(f32[8192]{0:T(1024)} %param.11) | copy-start | bytes 98308
  97.7 165.6 %all-reduce.7.cloned.1.call-start = ((), (), s32[]{:S(2)}) async-start(), calls=%async_computation.4 | async-start | bytes 1048576 | tf_op jit(solution)/shard_map/psum | solution.py:32
  187.4 17.1 %copy-start = (f32[64,16,128]{2,1,0:T(8,128)S(1)}, f32[64,16,128]{2,1,0:T(8,128)}, u32[]{:S(2)}) copy-start(f32[64,16,128]{2,1,0:T(8,128)} %reduce-scatter.2.cloned.1.call-done) | copy-start | bytes 1572868
Sparse Core Ops, SparseCore 0:
  9.5 19.4 all-gather.1
  31.9 33.3 all-reduce.4
  97.9 89.4 reduce-scatter.1
  190.6 72.6 all-reduce.6
